TPU v7x, 128 devices: a whole 4x4x4 slice. The times are simulated.
128 devices in a mesh: row: 16 (over x, z_lo, core), col: 8 (over z_hi, y).
Axes of the slice: x: 4, y: 4, z: 4 (z_hi: 2, z_lo: 2; z = z_hi * 2 + z_lo), core: 2. Of those that a mesh axis runs over, the one named last changes fastest.
Arguments:
- value_proj: float32 [16, 8, 1024, 512], P('row', 'col'), may hold values from -6 to 6
- token_pool: bfloat16 [16, 8, 1536, 1024], P('row', 'col'), may hold values from -6 to 6
- target_pool: bfloat16 [16, 8, 1536, 1024], P('row', 'col'), may hold values from -6 to 6
- batch_ids: int32 [16, 8, 3, 1536], P('row', 'col'), may hold values from 0 to 1535
- frozen_out: bfloat16 [512, 1024], replicated, may hold values from -0.25 to 0.25
- numerators: int32 [3], replicated, may hold values from 4 to 15
Outputs:
- final_proj: float32 [16, 8, 1024, 512], P('row', 'col')
- final_tracker: float32 [16, 8, 1024, 512], P('row', 'col')
All inputs are finite; a program needn't handle non-finite values.
Results may differ from a plain program's by a relative error of at most 0.017.
Values sent between devices are 32-bit elements; how exact they have to be, the bound alone decides.
A program may use at most 128 MiB of HBM per device.

v0:
```python
import jax
import jax.numpy as jnp
from jax import lax
from jax.sharding import PartitionSpec as P

ITERS = 2


step_rate = 0.2


def shifted(block, axis, distance):
    devices = range(lax.axis_size(axis))
    route = [((i - distance) % len(devices), i) for i in devices]
    return lax.ppermute(block, axis, route)


def local_gradient(current, pool_rows, target_rows, chosen, frozen_out):
    factor = pool_rows.shape[1] ** (-0.5)
    tokens = pool_rows[chosen]
    targets = target_rows[chosen]
    preact = (
        jnp.dot(tokens, current.astype(jnp.bfloat16), preferred_element_type=jnp.float32) * factor
    )
    sigmoid_pre = jax.nn.sigmoid(preact)
    hidden = (preact * sigmoid_pre).astype(jnp.bfloat16)
    output = jnp.dot(hidden, frozen_out, preferred_element_type=jnp.float32)
    error_term = (output - targets.astype(jnp.float32)).astype(jnp.bfloat16)
    back_hidden = lax.dot_general(
        error_term, frozen_out, (((1,), (1,)), ((), ())), preferred_element_type=jnp.float32
    )
    slope = sigmoid_pre * (1.0 + preact * (1.0 - sigmoid_pre))
    back_pre = (back_hidden * slope).astype(jnp.bfloat16)
    return (
        lax.dot_general(
            tokens, back_pre, (((0,), (0,)), ((), ())), preferred_element_type=jnp.float32
        )
        * factor
    )


def combine(mix_weights, own, from_row, from_col):
    return mix_weights[0] * own + mix_weights[1] * from_row + mix_weights[2] * from_col


def on_device(value_proj, token_pool, target_pool, batch_ids, frozen_out, numerators):
    counts = numerators.astype(jnp.float32)
    mix_weights = counts / jnp.sum(counts)
    current = value_proj[0, 0]
    pool_rows = token_pool[0, 0]
    target_rows = target_pool[0, 0]
    chosen_ids = batch_ids[0, 0]

    def gradient_at(field, which):
        return local_gradient(field, pool_rows, target_rows, chosen_ids[which], frozen_out)

    grad_old = gradient_at(current, 0)
    tracker = grad_old
    for which in range(1, ITERS + 1):
        from_row = shifted((current, tracker), "row", 1)
        from_col = shifted((current, tracker), "col", 1)
        mixed_proj = combine(mix_weights, current, from_row[0], from_col[0])
        mixed_track = combine(mix_weights, tracker, from_row[1], from_col[1])
        current = mixed_proj - step_rate * tracker
        grad_new = gradient_at(current, which)
        tracker = mixed_track + grad_new - grad_old
        grad_old = grad_new
    return (current[None, None], tracker[None, None])


def solution(mesh):
    return jax.shard_map(
        on_device,
        mesh=mesh,
        in_specs=(
            P("row", "col", None, None),
            P("row", "col", None, None),
            P("row", "col", None, None),
            P("row", "col", None, None),
            P(),
            P(),
        ),
        out_specs=(P("row", "col", None, None), P("row", "col", None, None)),
        check_vma=False,
    )
```

profile of v0, /device:TPU:1, one launch (start us, length us, event | category | flops | bytes accessed | tf_op | source)
XLA Modules:
  0.0 311.2 jit_solution(15108484111219045867)
XLA Ops:
  0.6 0.0 copy-start
  0.6 3.1 collective-permute-start
  3.7 1.3 collective-permute-start.1
  5.0 0.8 fusion.14
  5.8 1.3 convert_reduce_fusion
  7.1 1.3 convert_divide_fusion
  8.4 5.9 %gather_fusion = bf16[1536,1024]{1,0:T(8,128)(2,1)} fusion(bf16[1536,1024]{1,0:T(8,128)(2,1)S(1)} %bitcast.44, s32[2048]{0:T(1024)S(1)} %pad_clamp_fusion.2), kind=kCustom, calls=%fused_computation | custom fusion | bytes 6297600 | tf_op jit(solution)/shard_map/gather | solution.py:20
  14.3 10.1 %gather_fusion.1 = bf16[1536,1024]{1,0:T(8,128)(2,1)} fusion(bf16[1536,1024]{1,0:T(8,128)(2,1)} %bitcast.47, s32[2048]{0:T(1024)S(1)} %pad_clamp_fusion.2), kind=kCustom, calls=%fused_computation.1 | custom fusion | bytes 6297600 | tf_op jit(solution)/shard_map/gather | solution.py:21
  24.4 5.9 %gather_fusion.2 = bf16[1536,1024]{1,0:T(8,128)(2,1)} fusion(bf16[1536,1024]{1,0:T(8,128)(2,1)S(1)} %bitcast.45, s32[2048]{0:T(1024)S(1)} %get-tuple-element.14), kind=kCustom, calls=%fused_computation.2 | custom fusion | bytes 6297600 | tf_op jit(solution)/shard_map/gather | solution.py:20
  30.2 10.1 %gather_fusion.3 = bf16[1536,1024]{1,0:T(8,128)(2,1)} fusion(bf16[1536,1024]{1,0:T(8,128)(2,1)} %bitcast.48, s32[2048]{0:T(1024)S(1)} %get-tuple-element.14), kind=kCustom, calls=%fused_computation.3 | custom fusion | bytes 6297600 | tf_op jit(solution)/shard_map/gather | solution.py:21
  40.3 5.8 %gather_fusion.4 = bf16[1536,1024]{1,0:T(8,128)(2,1)} fusion(bf16[1536,1024]{1,0:T(8,128)(2,1)S(1)} %bitcast.46, s32[2048]{0:T(1024)S(1)} %get-tuple-element.13), kind=kCustom, calls=%fused_computation.4 | custom fusion | bytes 6297600 | tf_op jit(solution)/shard_map/gather | solution.py:20
  46.1 10.2 %gather_fusion.5 = bf16[1536,1024]{1,0:T(8,128)(2,1)} fusion(bf16[1536,1024]{1,0:T(8,128)(2,1)} %bitcast.49, s32[2048]{0:T(1024)S(1)} %get-tuple-element.13), kind=kCustom, calls=%fused_computation.5 | custom fusion | bytes 6297600 | tf_op jit(solution)/shard_map/gather | solution.py:21
  56.4 0.6 fusion.23
  57.6 5.0 %convolution_multiply_fusion.5 = f32[1536,512]{1,0:T(8,128)} fusion(bf16[1536,1024]{1,0:T(8,128)(2,1)S(1)} %copy-done.2, f32[1,1,1024,512]{3,2,1,0:T(8,128)} %param.6), kind=kOutput, calls=%fused_computation.14 | convolution fusion | flops 1611399168 | bytes 8388608 | tf_op jit(solution)/shard_map/dot_general | solution.py:23
  62.7 9.9 %fusion = bf16[1536,512]{1,0:T(8,128)(2,1)} fusion(f32[1536,512]{1,0:T(8,128)} %convolution_multiply_fusion.5, bf16[512,1024]{1,0:T(8,128)(2,1)} %param.10, bf16[1536,1024]{1,0:T(8,128)(2,1)} %gather_fusion.1), kind=kOutput, calls=%fused_computation.21 | convolution fusion | flops 3236954112 | bytes 8912896 | tf_op jit(solution)/shard_map/dot_general | solution.py:29
  72.6 10.2 %broadcast_multiply_fusion = (f32[1024,512]{1,0:T(8,128)}, f32[1024,512]{1,0:T(8,128)}, f32[1024,512]{1,0:T(8,128)}) fusion(f32[1024,512]{1,0:T(8,128)} %collective-permute-done.1, f32[]{:T(128)} %bitcast.3, f32[1024,512]{1,0:T(8,128)} %collective-permute-done, f32[]{:T(128)} %bitcast.2, f32[1,1,1024,512]{3,2,1,0:T(8,128)} %param.6, f32[]{:T(128)} %bitcast, ...), kind=kOutput, calls=%fused_computation.33 | convolution fusion | flops 1614807040 | bytes 17301516 | tf_op jit(solution)/shard_map/dot_general | solution.py:35
  82.8 4.9 %collective-permute-start.2 = (f32[1024,512]{1,0:T(8,128)}, f32[1024,512]{1,0:T(8,128)}, u32[]{:S(2)}, u32[]{:S(2)}) collective-permute-start(f32[1024,512]{1,0:T(8,128)} %get-tuple-element.8), channel_id=1, source_target_pairs={{120,0},{0,8},{8,16},{16,24},{24,32},{32,40},{40,48},{48,56},{56,6... | collective-permute-start | bytes 6291464 | tf_op jit(solution)/shard_map/ppermute | solution.py:15
  87.7 0.3 collective-permute-start.4
  88.0 0.0 collective-permute-start.5
  88.0 5.2 %convolution_multiply_fusion.3 = f32[1536,512]{1,0:T(8,128)} fusion(bf16[1536,1024]{1,0:T(8,128)(2,1)S(1)} %copy-done.8, f32[1024,512]{1,0:T(8,128)} %get-tuple-element.8), kind=kOutput, calls=%fused_computation.12 | convolution fusion | flops 1611923456 | bytes 8388608 | tf_op jit(solution)/shard_map/dot_general | solution.py:23
  93.2 8.9 %fusion.1 = bf16[1536,512]{1,0:T(8,128)(2,1)} fusion(f32[1536,512]{1,0:T(8,128)} %convolution_multiply_fusion.3, bf16[512,1024]{1,0:T(8,128)(2,1)} %param.10, bf16[1536,1024]{1,0:T(8,128)(2,1)S(1)} %copy-done.9), kind=kOutput, calls=%fused_computation.22 | convolution fusion | flops 3236954112 | bytes 8912896 | tf_op jit(solution)/shard_map/dot_general | solution.py:29
  102.1 4.3 %fusion.26 = f32[1024,512]{1,0:T(8,128)S(1)} fusion(bf16[1536,1024]{1,0:T(8,128)(2,1)} %gather_fusion.2, bf16[1536,512]{1,0:T(8,128)(2,1)} %fusion.1), kind=kOutput, calls=%fused_computation.52 | convolution fusion | flops 1610612736 | bytes 6815744 | tf_op jit(solution)/shard_map/dot_general | solution.py:35
  106.5 94.4 %collective-permute-done.2 = f32[1024,512]{1,0:T(8,128)} collective-permute-done((f32[1024,512]{1,0:T(8,128)}, f32[1024,512]{1,0:T(8,128)}, u32[]{:S(2)}, u32[]{:S(2)}) %collective-permute-start.2) | collective-permute-done | bytes 2097184 | tf_op jit(solution)/shard_map/ppermute | solution.py:15
  200.8 22.5 %collective-permute-done.4 = f32[1024,512]{1,0:T(8,128)} collective-permute-done((f32[1024,512]{1,0:T(8,128)}, f32[1024,512]{1,0:T(8,128)}, u32[]{:S(2)}, u32[]{:S(2)}) %collective-permute-start.4) | collective-permute-done | bytes 2097184 | tf_op jit(solution)/shard_map/ppermute | solution.py:15
  223.3 9.4 %multiply_subtract_fusion = (f32[1024,512]{1,0:T(8,128)S(1)}, f32[1024,512]{1,0:T(8,128)}) fusion(f32[1024,512]{1,0:T(8,128)} %collective-permute-done.3, f32[1024,512]{1,0:T(8,128)} %collective-permute-done.2, f32[1024,512]{1,0:T(8,128)} %get-tuple-element.8, f32[]{:T(128)} %bitcast.3, f32[]{:T(128)} %bitcast.2, f32[]{:T(128)} %bitcast, ...), kind=kLoop, calls=%fused_computation.25 | loop fusion | flops 8388608 | bytes 18874384 | tf_op jit(solution)/shard_map/sub | solution.py:64
  232.8 2.5 collective-permute-start.6
  235.3 0.0 collective-permute-start.7
  235.3 3.6 %convolution_multiply_fusion.1 = f32[1536,512]{1,0:T(8,128)} fusion(bf16[1536,1024]{1,0:T(8,128)(2,1)S(1)} %copy-done.6, f32[1024,512]{1,0:T(8,128)S(1)} %get-tuple-element.5), kind=kOutput, calls=%fused_computation.10 | convolution fusion | flops 1611923456 | bytes 8388608 | tf_op jit(solution)/shard_map/dot_general | solution.py:23
  238.8 10.0 %fusion.2 = bf16[1536,512]{1,0:T(8,128)(2,1)} fusion(f32[1536,512]{1,0:T(8,128)} %convolution_multiply_fusion.1, bf16[512,1024]{1,0:T(8,128)(2,1)} %param.10, bf16[1536,1024]{1,0:T(8,128)(2,1)} %gather_fusion.5), kind=kOutput, calls=%fused_computation.23 | convolution fusion | flops 3236954112 | bytes 8912896 | tf_op jit(solution)/shard_map/dot_general | solution.py:29
  248.8 3.4 %fusion.27 = f32[1024,512]{1,0:T(8,128)S(1)} fusion(bf16[1536,1024]{1,0:T(8,128)(2,1)S(1)} %copy-done.7, bf16[1536,512]{1,0:T(8,128)(2,1)} %fusion.2), kind=kOutput, calls=%fused_computation.53 | convolution fusion | flops 1610612736 | bytes 6815744 | tf_op jit(solution)/shard_map/dot_general | solution.py:35
  252.2 51.3 %collective-permute-done.6 = f32[1024,512]{1,0:T(8,128)} collective-permute-done((f32[1024,512]{1,0:T(8,128)}, f32[1024,512]{1,0:T(8,128)}, u32[]{:S(2)}, u32[]{:S(2)}) %collective-permute-start.6) | collective-permute-done | bytes 2097184 | tf_op jit(solution)/shard_map/ppermute | solution.py:15
  303.5 7.7 %subtract_bitcast_fusion = f32[1,1,1024,512]{3,2,1,0:T(8,128)} fusion(f32[1024,512]{1,0:T(8,128)S(1)} %fusion.27, f32[1024,512]{1,0:T(8,128)} %collective-permute-done.7, f32[1024,512]{1,0:T(8,128)} %collective-permute-done.6, f32[1024,512]{1,0:T(8,128)} %get-tuple-element.6, f32[1024,512]{1,0:T(8,128)S(1)} %copy-done.5, f32[]{:T(128)} %bitcast.3, ...), kind=kLoop, calls=%fused_computation.24 | loop fusion | flops 4718592 | bytes 12582924 | tf_op jit(solution)/shard_map/broadcast_in_dim | solution.py:68
  (29 shorter events, 0.1 us)
Async XLA Ops:
  0.6 7.8 %copy-start = (bf16[1,1,1536,1024]{3,2,1,0:T(8,128)(2,1)S(1)}, bf16[1,1,1536,1024]{3,2,1,0:T(8,128)(2,1)}, u32[]{:S(2)}) copy-start(bf16[1,1,1536,1024]{3,2,1,0:T(8,128)(2,1)} %param.7) | copy-start | bytes 9437188
  0.6 71.9 %collective-permute-start = (f32[1024,512]{1,0:T(8,128)}, f32[1024,512]{1,0:T(8,128)}, u32[]{:S(2)}, u32[]{:S(2)}) collective-permute-start(f32[1024,512]{1,0:T(8,128)} %bitcast.50), channel_id=1, source_target_pairs={{120,0},{0,8},{8,16},{16,24},{24,32},{32,40},{40,48},{48,56},{56,6... | collective-permute-start | bytes 6291464 | tf_op jit(solution)/shard_map/ppermute | solution.py:15
  3.7 68.8 %collective-permute-start.1 = (f32[1024,512]{1,0:T(8,128)}, f32[1024,512]{1,0:T(8,128)}, u32[]{:S(2)}, u32[]{:S(2)}) collective-permute-start(f32[1024,512]{1,0:T(8,128)} %bitcast.51), channel_id=1, source_target_pairs={{7,0},{0,1},{1,2},{2,3},{3,4},{4,5},{5,6},{6,7},{15,8},{8,9},{9,10... | collective-permute-start | bytes 6291464 | tf_op jit(solution)/shard_map/ppermute | solution.py:15
  46.1 11.5 %copy-start.2 = (bf16[1536,1024]{1,0:T(8,128)(2,1)S(1)}, bf16[1536,1024]{1,0:T(8,128)(2,1)}, u32[]{:S(2)}) copy-start(bf16[1536,1024]{1,0:T(8,128)(2,1)} %gather_fusion) | copy-start | bytes 9437188
  72.6 15.4 %copy-start.8 = (bf16[1536,1024]{1,0:T(8,128)(2,1)S(1)}, bf16[1536,1024]{1,0:T(8,128)(2,1)}, u32[]{:S(2)}) copy-start(bf16[1536,1024]{1,0:T(8,128)(2,1)} %gather_fusion.2) | copy-start | bytes 9437188
  82.8 118.0 %collective-permute-start.2 = (f32[1024,512]{1,0:T(8,128)}, f32[1024,512]{1,0:T(8,128)}, u32[]{:S(2)}, u32[]{:S(2)}) collective-permute-start(f32[1024,512]{1,0:T(8,128)} %get-tuple-element.8), channel_id=1, source_target_pairs={{120,0},{0,8},{8,16},{16,24},{24,32},{32,40},{40,48},{48,56},{56,6... | collective-permute-start | bytes 6291464 | tf_op jit(solution)/shard_map/ppermute | solution.py:15
  87.7 113.2 %collective-permute-start.3 = (f32[1024,512]{1,0:T(8,128)}, f32[1024,512]{1,0:T(8,128)}, u32[]{:S(2)}, u32[]{:S(2)}) collective-permute-start(f32[1024,512]{1,0:T(8,128)} %get-tuple-element.8), channel_id=1, source_target_pairs={{7,0},{0,1},{1,2},{2,3},{3,4},{4,5},{5,6},{6,7},{15,8},{8,9},{9,10... | collective-permute-start | bytes 6291464 | tf_op jit(solution)/shard_map/ppermute | solution.py:15
  87.7 5.5 %copy-start.9 = (bf16[1536,1024]{1,0:T(8,128)(2,1)S(1)}, bf16[1536,1024]{1,0:T(8,128)(2,1)}, u32[]{:S(2)}) copy-start(bf16[1536,1024]{1,0:T(8,128)(2,1)} %gather_fusion.3) | copy-start | bytes 9437188
  87.7 135.6 %collective-permute-start.4 = (f32[1024,512]{1,0:T(8,128)}, f32[1024,512]{1,0:T(8,128)}, u32[]{:S(2)}, u32[]{:S(2)}) collective-permute-start(f32[1024,512]{1,0:T(8,128)} %get-tuple-element.7), channel_id=1, source_target_pairs={{120,0},{0,8},{8,16},{16,24},{24,32},{32,40},{40,48},{48,56},{56,6... | collective-permute-start | bytes 6291464 | tf_op jit(solution)/shard_map/ppermute | solution.py:15
  88.0 135.3 %collective-permute-start.5 = (f32[1024,512]{1,0:T(8,128)}, f32[1024,512]{1,0:T(8,128)}, u32[]{:S(2)}, u32[]{:S(2)}) collective-permute-start(f32[1024,512]{1,0:T(8,128)} %get-tuple-element.7), channel_id=1, source_target_pairs={{7,0},{0,1},{1,2},{2,3},{3,4},{4,5},{5,6},{6,7},{15,8},{8,9},{9,10... | collective-permute-start | bytes 6291464 | tf_op jit(solution)/shard_map/ppermute | solution.py:15
  102.1 121.2 %copy-start.3 = (f32[1024,512]{1,0:T(8,128)S(1)}, f32[1024,512]{1,0:T(8,128)}, u32[]{:S(2)}) copy-start(f32[1024,512]{1,0:T(8,128)} %get-tuple-element.12) | copy-start | bytes 6291460
  106.5 126.3 %copy-start.4 = (f32[1024,512]{1,0:T(8,128)}, f32[1024,512]{1,0:T(8,128)S(1)}, u32[]{:S(2)}) copy-start(f32[1024,512]{1,0:T(8,128)S(1)} %fusion.26) | copy-start | bytes 6291460
  223.3 11.9 %copy-start.6 = (bf16[1536,1024]{1,0:T(8,128)(2,1)S(1)}, bf16[1536,1024]{1,0:T(8,128)(2,1)}, u32[]{:S(2)}) copy-start(bf16[1536,1024]{1,0:T(8,128)(2,1)} %gather_fusion.4) | copy-start | bytes 9437188
  232.8 2.5 copy-start.10
  232.8 70.7 %collective-permute-start.6 = (f32[1024,512]{1,0:T(8,128)}, f32[1024,512]{1,0:T(8,128)}, u32[]{:S(2)}, u32[]{:S(2)}) collective-permute-start(f32[1024,512]{1,0:T(8,128)} %get-tuple-element.6), channel_id=1, source_target_pairs={{120,0},{0,8},{8,16},{16,24},{24,32},{32,40},{40,48},{48,56},{56,6... | collective-permute-start | bytes 6291464 | tf_op jit(solution)/shard_map/ppermute | solution.py:15
  235.3 68.2 %collective-permute-start.7 = (f32[1024,512]{1,0:T(8,128)}, f32[1024,512]{1,0:T(8,128)}, u32[]{:S(2)}, u32[]{:S(2)}) collective-permute-start(f32[1024,512]{1,0:T(8,128)} %get-tuple-element.6), channel_id=1, source_target_pairs={{7,0},{0,1},{1,2},{2,3},{3,4},{4,5},{5,6},{6,7},{15,8},{8,9},{9,10... | collective-permute-start | bytes 6291464 | tf_op jit(solution)/shard_map/ppermute | solution.py:15
  238.8 10.0 %copy-start.7 = (bf16[1536,1024]{1,0:T(8,128)(2,1)S(1)}, bf16[1536,1024]{1,0:T(8,128)(2,1)}, u32[]{:S(2)}) copy-start(bf16[1536,1024]{1,0:T(8,128)(2,1)} %gather_fusion.4) | copy-start | bytes 9437188
  248.8 54.7 %copy-start.5 = (f32[1024,512]{1,0:T(8,128)S(1)}, f32[1024,512]{1,0:T(8,128)}, u32[]{:S(2)}) copy-start(f32[1024,512]{1,0:T(8,128)} %copy-done.4) | copy-start | bytes 6291460
  303.5 7.7 %copy-start.1 = (bf16[1,1,1536,1024]{3,2,1,0:T(8,128)(2,1)S(1)}, bf16[1,1,1536,1024]{3,2,1,0:T(8,128)(2,1)}, u32[]{:S(2)}) copy-start(bf16[1,1,1536,1024]{3,2,1,0:T(8,128)(2,1)} %param.7) | copy-start | bytes 9437188
where the time goes:
time: 312 us; the launch traced here: 311 us
  waiting for transfers between devices  168 us (54%)
  matrix products  60.5 us (19%)
  local copies, waits for them, and re-layouts  48.6 us (16%)
  other arithmetic  20.5 us (7%)
  starting transfers between devices  12 us (4%)
    ppermute x8, waiting for transfers between devices, shifted(): return lax.ppermute(block, axis, route)  168 us
    gather x3, local copies, waits for them, and re-layouts, local_gradient(): targets = target_rows[chosen]  30.4 us
    dot_general x3, matrix products, local_gradient(): lax.dot_general(error_term, frozen_out, (((1,), (1,)), ((), ())), preferr...  28.8 us
    dot_general x3, matrix products, local_gradient(): lax.dot_general(tokens, back_pre, (((0,), (0,)), ((), ())), preferred_ele...  17.9 us
    gather x3, local copies, waits for them, and re-layouts, local_gradient(): tokens = pool_rows[chosen]  17.5 us
    dot_general x3, matrix products, local_gradient(): jnp.dot(tokens, current.astype(jnp.bfloat16), preferred_element_type=jnp....  13.8 us
    ppermute x8, starting transfers between devices, shifted(): return lax.ppermute(block, axis, route)  12 us
    sub x1, other arithmetic, on_device(): current = mixed_proj - step_rate * tracker  9.44 us
  transfers between devices with their start and end apart: 8, of which 3 were waited for; matrix products, arithmetic and copies ran while one was open for 33% of the time, Pallas kernels for 0%

commit v1 on v0

v1 whole, which is shorter than its diff:
```python
import functools

import jax
import jax.numpy as jnp
from jax import lax
from jax.experimental import pallas as pl
from jax.experimental.pallas import tpu as pltpu
from jax.sharding import PartitionSpec as P

MESH = pl.DeviceIdType.MESH
F32 = jnp.float32
BF16 = jnp.bfloat16
STEP = 0.2
LANES = 128
TILE = 256


def kernel(
    num_ref, x_hbm, tok_hbm, tgt_hbm, ids_ref, fro_hbm,
    xo_hbm, to_hbm,
    xs, xr, xc, xa, xx, ws, wr, g0, gr, gc, g1, ts, tr, tc, q, g2,
    x_relay, g_relay, t_relay,
    tok, tgt, tokt, fro, frot, bp, xb,
    load_sem, x_sem, out_sem,
    xr_s, xr_r, xc_s, xc_r, xa_s, xa_r, xx_s, xx_r, wr_s, wr_r,
    gr_s, gr_r, gc_s, gc_r, tr_s, tr_r, tc_s, tc_r,
    rel_s, rel_r,
):
    chunks, rows, _ = xs.shape
    n_pool, depth = tok.shape
    heads = fro.shape[0]
    factor = depth ** -0.5

    r, c = lax.axis_index("row"), lax.axis_index("col")
    y, half = lax.rem(c, 4), 4 * (c // 4)
    seam = y == 3
    row_next = (lax.rem(r + 1, 16), c)
    row_prev = (lax.rem(r + 15, 16), c)
    col_next = (r, lax.rem(c + 1, 8))
    swap = (r, lax.rem(c + 4, 8))
    up = (r, half + lax.rem(y + 1, 4))
    down = (r, half + lax.rem(y + 3, 4))
    up_swap = (r, lax.rem(up[1] + 4, 8))
    down_swap = (r, lax.rem(down[1] + 4, 8))
    two_first = (r, jnp.where(y >= 2, down_swap[1], down[1]))

    loads = [
        pltpu.make_async_copy(x_hbm.at[0, 0, :, pl.ds(i * LANES, LANES)], xs.at[i], x_sem.at[i])
        for i in range(chunks)
    ]
    for load in loads:
        load.start()
    tok_load = pltpu.make_async_copy(tok_hbm.at[0, 0], tok, load_sem.at[0])
    fro_load = pltpu.make_async_copy(fro_hbm, fro, load_sem.at[1])
    tgt_load = pltpu.make_async_copy(tgt_hbm.at[0, 0], tgt, load_sem.at[2])
    tok_load.start()
    fro_load.start()
    tgt_load.start()

    barrier = pltpu.get_barrier_semaphore()
    partners = (row_next, row_prev, up, down, swap, up_swap, down_swap)
    for partner in partners:
        pl.semaphore_signal(barrier, inc=1, device_id=partner, device_id_type=MESH)
    pl.semaphore_wait(barrier, len(partners))

    def remote(src, dst, send, recv, i, device, j=None):
        return pltpu.make_async_remote_copy(
            src_ref=src.at[i], dst_ref=dst.at[i if j is None else j], send_sem=send.at[i],
            recv_sem=recv.at[i], device_id=device, device_id_type=MESH,
        )

    def relayed(i):
        return i % 2 == 1

    def swap_copy(src, relay, which, send, i):
        return pltpu.make_async_remote_copy(
            src_ref=src.at[i], dst_ref=relay.at[i // 2], send_sem=send.at[i],
            recv_sem=rel_r.at[which, i // 2], device_id=swap, device_id_type=MESH,
        )

    def forward_copy(relay, which, dst, recv, i):
        return pltpu.make_async_remote_copy(
            src_ref=relay.at[i // 2], dst_ref=dst.at[i], send_sem=rel_s.at[which, i // 2],
            recv_sem=recv.at[i], device_id=up, device_id_type=MESH,
        )

    def send_swaps(src, relay, which, send, i):
        if relayed(i):
            @pl.when(seam)
            def _():
                swap_copy(src, relay, which, send, i).start()

    def send_col(src, dst, send, recv, i):
        copy = remote(src, dst, send, recv, i, col_next)
        if relayed(i):
            pl.when(jnp.logical_not(seam))(copy.start)
        else:
            copy.start()

    def forward(src, relay, which, dst, send, recv, i):
        if relayed(i):
            @pl.when(seam)
            def _():
                swap_copy(src, relay, which, send, i).wait_recv()
                forward_copy(relay, which, dst, recv, i).start()

    for i in range(chunks):
        loads[i].wait()
        send_swaps(xs, x_relay, 0, xc_s, i)
        send_col(xs, xc, xc_s, xc_r, i)
    for i in range(chunks):
        remote(xs, xr, xr_s, xr_r, i, row_next).start()
    for i in range(chunks):
        remote(xs, xa, xa_s, xa_r, i, two_first).start()

    weights = [jnp.full((1, LANES), num_ref[i].astype(F32), F32) for i in range(3)]
    total = weights[0] + weights[1] + weights[2]
    own, by_row, by_col = (w / total for w in weights)

    def over(i, body):
        def step(t, carry):
            body(pl.ds(pl.multiple_of(t * LANES, LANES), LANES))
            return carry

        lax.fori_loop(0, rows // LANES, step, 0)

    def gradient(which, out):
        def tile(t, carry):
            at = pl.ds(pl.multiple_of(t * TILE, TILE), TILE)
            pre = jnp.dot(tok[at, :], xb[...], preferred_element_type=F32) * factor
            sig = jax.nn.sigmoid(pre)
            hidden = (pre * sig).astype(BF16)
            slope = sig * (1.0 + pre * (1.0 - sig))
            output = jnp.dot(hidden, fro[...], preferred_element_type=F32)
            err = (output - tgt[at, :].astype(F32)).astype(BF16)
            back = jnp.dot(err, frot[...], preferred_element_type=F32)
            place = t * TILE + lax.broadcasted_iota(jnp.int32, (TILE, LANES), 0)
            drawn = jnp.zeros((TILE, LANES), F32)
            for l in range(ids_ref.shape[3] // LANES):
                ids = ids_ref[0, 0, which : which + 1, l * LANES : (l + 1) * LANES]
                drawn += jnp.where(ids == place, 1.0, 0.0)
            drawn = jnp.sum(drawn, axis=1, keepdims=True)
            bp[at, :] = (back * slope * drawn).astype(BF16)
            return carry

        lax.fori_loop(0, n_pool // TILE, tile, 0)

        def block(t, carry):
            at = pl.ds(pl.multiple_of(t * TILE, TILE), TILE)
            for n in range(heads // TILE):
                g = jnp.dot(tokt[at, :], bp[:, n * TILE : (n + 1) * TILE], preferred_element_type=F32) * factor
                for l in range(TILE // LANES):
                    out[n * (TILE // LANES) + l, at, :] = g[:, l * LANES : (l + 1) * LANES]
            return carry

        lax.fori_loop(0, depth // TILE, block, 0)

    def cols(i):
        return slice(i * LANES, (i + 1) * LANES)

    for i in range(chunks):
        def cast(at, i=i):
            xb[at, cols(i)] = xs[i, at, :].astype(BF16)
        over(i, cast)
    tok_load.wait()

    def turn(t, carry):
        at = pl.ds(pl.multiple_of(t * TILE, TILE), TILE)
        tokt[:, at] = tok[at, :].T
        return carry

    lax.fori_loop(0, n_pool // TILE, turn, 0)
    fro_load.wait()
    for t in range(heads // TILE):
        frot[:, t * TILE : (t + 1) * TILE] = fro[t * TILE : (t + 1) * TILE, :].T
    tgt_load.wait()
    gradient(0, g0)

    for i in range(chunks):
        send_swaps(g0, g_relay, 1, gc_s, i)
    for i in range(chunks):
        remote(g0, gr, gr_s, gr_r, i, row_next).start()
    for i in range(chunks):
        forward(xs, x_relay, 0, xc, xc_s, xc_r, i)
    for i in range(chunks):
        send_col(g0, gc, gc_s, gc_r, i)

    def pass_on(i):
        remote(xs, xa, xa_s, xa_r, i, two_first).wait_recv()
        remote(xa, xx, xx_s, xx_r, i, down).start()

    for i in range(chunks // 2):
        pass_on(i)

    for i in range(chunks):
        remote(xs, xc, xc_s, xc_r, i, col_next).wait_recv()
        remote(xs, xr, xr_s, xr_r, i, row_next).wait_recv()

        def first(at, i=i):
            from_col = by_col * xc[i, at, :]
            mixed = own * xs[i, at, :] + by_row * xr[i, at, :] + from_col
            ws[i, at, :] = mixed + from_col
            xb[at, cols(i)] = (mixed - STEP * g0[i, at, :]).astype(BF16)

        over(i, first)
        remote(ws, wr, wr_s, wr_r, i, row_next).start()
    gradient(1, g1)

    for i in range(chunks // 2, chunks):
        pass_on(i)
    for i in range(chunks):
        forward(g0, g_relay, 1, gc, gc_s, gc_r, i)

    for i in range(chunks):
        remote(g0, gc, gc_s, gc_r, i, col_next).wait_recv()
        remote(g0, gr, gr_s, gr_r, i, row_next).wait_recv()

        def second(at, i=i):
            g = g0[i, at, :]
            mixed = own * g + by_row * gr[i, at, :] + by_col * gc[i, at, :]
            track = (mixed + g1[i, at, :]) - g
            ts[i, at, :] = track
            q[i, at, :] = STEP * (mixed + track)

        over(i, second)
        send_swaps(ts, t_relay, 2, tc_s, i)
        send_col(ts, tc, tc_s, tc_r, i)
        remote(ts, tr, tr_s, tr_r, i, row_next).start()

    outs = []
    for i in range(chunks):
        remote(ws, wr, wr_s, wr_r, i, row_next).wait_recv()
        remote(xa, xx, xx_s, xx_r, i, down).wait_recv()

        def third(at, i=i):
            new = own * ws[i, at, :] + by_row * wr[i, at, :] + (by_col * by_col) * xx[i, at, :] - q[i, at, :]
            q[i, at, :] = new
            xb[at, cols(i)] = new.astype(BF16)

        over(i, third)
        out = pltpu.make_async_copy(q.at[i], xo_hbm.at[0, 0, :, pl.ds(i * LANES, LANES)], out_sem.at[0, i])
        out.start()
        outs.append(out)
    gradient(2, g2)

    for i in range(chunks):
        forward(ts, t_relay, 2, tc, tc_s, tc_r, i)

    for i in range(chunks):
        remote(ts, tc, tc_s, tc_r, i, col_next).wait_recv()
        remote(ts, tr, tr_s, tr_r, i, row_next).wait_recv()

        def last(at, i=i):
            mixed = own * ts[i, at, :] + by_row * tr[i, at, :] + by_col * tc[i, at, :]
            g2[i, at, :] = (mixed + g2[i, at, :]) - g1[i, at, :]

        over(i, last)
        out = pltpu.make_async_copy(g2.at[i], to_hbm.at[0, 0, :, pl.ds(i * LANES, LANES)], out_sem.at[1, i])
        out.start()
        outs.append(out)

    for i in range(chunks):
        remote(xs, xc, xc_s, xc_r, i, col_next).wait_send()
        remote(xs, xr, xr_s, xr_r, i, row_next).wait_send()
        remote(xs, xa, xa_s, xa_r, i, two_first).wait_send()
        remote(xa, xx, xx_s, xx_r, i, down).wait_send()
        remote(ws, wr, wr_s, wr_r, i, row_next).wait_send()
        remote(g0, gc, gc_s, gc_r, i, col_next).wait_send()
        remote(g0, gr, gr_s, gr_r, i, row_next).wait_send()
        remote(ts, tc, tc_s, tc_r, i, col_next).wait_send()
        remote(ts, tr, tr_s, tr_r, i, row_next).wait_send()
        if relayed(i):
            @pl.when(seam)
            def _():
                forward_copy(x_relay, 0, xc, xc_r, i).wait_send()
                forward_copy(g_relay, 1, gc, gc_r, i).wait_send()
                forward_copy(t_relay, 2, tc, tc_r, i).wait_send()
    for out in outs:
        out.wait()


def on_device(value_proj, token_pool, target_pool, batch_ids, frozen_out, numerators):
    depth, heads = value_proj.shape[2:]
    n_pool = token_pool.shape[2]
    chunks = heads // LANES
    field = pltpu.VMEM((chunks, depth, LANES), F32)
    relay = pltpu.VMEM((chunks // 2, depth, LANES), F32)
    dma = pltpu.SemaphoreType.DMA
    out = jax.ShapeDtypeStruct(value_proj.shape, F32)
    hbm = pl.BlockSpec(memory_space=pl.ANY)
    return pl.pallas_call(
        kernel,
        out_shape=(out, out),
        in_specs=[
            pl.BlockSpec(memory_space=pltpu.SMEM), hbm, hbm, hbm,
            pl.BlockSpec(memory_space=pltpu.VMEM), hbm,
        ],
        out_specs=(hbm, hbm),
        scratch_shapes=[field] * 16 + [relay] * 3 + [
            pltpu.VMEM((n_pool, depth), BF16),
            pltpu.VMEM((n_pool, depth), BF16),
            pltpu.VMEM((depth, n_pool), BF16),
            pltpu.VMEM((heads, depth), BF16),
            pltpu.VMEM((depth, heads), BF16),
            pltpu.VMEM((n_pool, heads), BF16),
            pltpu.VMEM((depth, heads), BF16),
            dma((3,)), dma((chunks,)), dma((2, chunks)),
        ] + [dma((chunks,))] * 18 + [dma((3, chunks // 2))] * 2,
        compiler_params=pltpu.CompilerParams(
            collective_id=0, has_side_effects=True, vmem_limit_bytes=67043328,
        ),
    )(numerators, value_proj, token_pool, target_pool, batch_ids, frozen_out)


def solution(mesh):
    return jax.shard_map(
        on_device,
        mesh=mesh,
        in_specs=(
            P("row", "col", None, None),
            P("row", "col", None, None),
            P("row", "col", None, None),
            P("row", "col", None, None),
            P(),
            P(),
        ),
        out_specs=(P("row", "col", None, None), P("row", "col", None, None)),
        check_vma=False,
    )
```

time: 312 us -> 207 us (0.66)
  the two profiles are of different devices: /device:TPU:1 before, /device:TPU:34 now
where the time goes in v1:
time: 207 us
  Pallas kernels  200 us (97%)
  local copies, waits for them, and re-layouts  5.89 us (3%)
    pallas_call x1, Pallas kernels, on_device(): pl.pallas_call(kernel, out_shape=(out, out), in_specs=[pl.BlockSpec(memor...  200 us
    unnamed x5, local copies, waits for them, and re-layouts  5.89 us

profile of v1, /device:TPU:34, one launch (start us, length us, event | category | flops | bytes accessed | tf_op | source)
XLA Modules:
  0.0 207.0 jit_solution(17771875184005342038)
XLA Ops:
  0.6 1.3 copy.8.ids_ref
  2.0 200.5 %shard_map.77 = (f32[1,1,1024,512]{3,2,1,0:T(8,128)}, f32[1,1,1024,512]{3,2,1,0:T(8,128)}) custom-call(s32[3]{0:T(128)} %num_ref.1, f32[1,1,1024,512]{3,2,1,0:T(8,128)} %x_hbm.1, bf16[1,1,1536,1024]{3,2,1,0:T(8,128)(2,1)} %tok_hbm.1, bf16[1,1,1536,1024]{3,2,1,0:T(8,128)(2,1)} %tgt_hbm.1, s32[1,1,3,1536]{3,2,1,0:T(4,128)} %copy.8.ids_ref, ...), custom_call_target="tpu_custom_call" | custom-call | tf_op jit(solution)/shard_map/pallas_call | solution.py:291
  202.4 0.0 copy-start
  202.4 3.2 %copy.11 = f32[1,1,1024,512]{3,2,1,0:T(8,128)} copy(f32[1,1,1024,512]{3,2,1,0:T(8,128)} %get-tuple-element.4) | data formatting | bytes 4194304
  205.7 0.0 copy-done
  205.7 1.3 copy.12
Async XLA Ops:
  202.4 3.2 %copy-start = (f32[1,1,1024,512]{3,2,1,0:T(8,128)S(1)}, f32[1,1,1024,512]{3,2,1,0:T(8,128)}, u32[]{:S(2)}) copy-start(f32[1,1,1024,512]{3,2,1,0:T(8,128)} %get-tuple-element.5) | copy-start | bytes 6291460

commit v2 on v1

v2 whole, which is shorter than its diff:
```python
import functools

import jax
import jax.numpy as jnp
from jax import lax
from jax.experimental import pallas as pl
from jax.experimental.pallas import tpu as pltpu
from jax.sharding import PartitionSpec as P

MESH = pl.DeviceIdType.MESH
F32 = jnp.float32
BF16 = jnp.bfloat16
STEP = 0.2
SPLIT = 2
LANES = 128
TILE = 256


def kernel(
    num_ref, x_hbm, tok_hbm, tgt_hbm, ids_hbm, fro_hbm,
    xo, to,
    xs, xr, xc, xa, xx, ws, wr, g0, gr, gc, g1, ts, tr, tc, q,
    x_relay, g_relay, t_relay,
    tok, tgt, tokt, fro, frot, bp, xb, ids_ref,
    load_sem, x_sem,
    xr_s, xr_r, xc_s, xc_r, xa_s, xa_r, xx_s, xx_r, wr_s, wr_r,
    gr_s, gr_r, gc_s, gc_r, tr_s, tr_r, tc_s, tc_r,
    rel_s, rel_r,
):
    chunks, rows, _ = xs.shape
    split = tok.shape[1] // rows
    scope = jax.named_scope
    n_pool, depth = tok.shape
    heads = fro.shape[0]
    factor = depth ** -0.5

    r, c = lax.axis_index("row"), lax.axis_index("col")
    y, half = lax.rem(c, 4), 4 * (c // 4)
    seam = y == 3
    plain = jnp.logical_not(seam)
    inner = jnp.logical_or(y == 1, y == 2)
    outer = jnp.logical_not(inner)
    through = jnp.logical_and(seam, lax.rem(r, 4) >= 2)
    landing = y == 0
    direct = jnp.logical_and(seam, jnp.logical_not(through))
    row_next = (lax.rem(r + 1, 16), c)
    row_prev = (lax.rem(r + 15, 16), c)
    col_next = (r, lax.rem(c + 1, 8))
    swap = (r, lax.rem(c + 4, 8))
    up = (r, half + lax.rem(y + 1, 4))
    down = (r, half + lax.rem(y + 3, 4))
    up_swap = (r, lax.rem(up[1] + 4, 8))
    down_swap = (r, lax.rem(down[1] + 4, 8))
    two_first = (r, jnp.where(y >= 2, down_swap[1], down[1]))

    def window(ref, i):
        return ref.at[0, 0, pl.ds((i % split) * rows, rows), pl.ds((i // split) * LANES, LANES)]

    loads = [
        pltpu.make_async_copy(window(x_hbm, i), xs.at[i], x_sem.at[i])
        for i in range(chunks)
    ]
    for load in loads:
        load.start()
    tok_load = pltpu.make_async_copy(tok_hbm.at[0, 0], tok, load_sem.at[0])
    fro_load = pltpu.make_async_copy(fro_hbm, fro, load_sem.at[1])
    tgt_load = pltpu.make_async_copy(tgt_hbm.at[0, 0], tgt, load_sem.at[2])
    ids_load = pltpu.make_async_copy(ids_hbm, ids_ref, load_sem.at[3])
    ids_load.start()
    tok_load.start()
    fro_load.start()
    tgt_load.start()

    barrier = pltpu.get_barrier_semaphore()
    partners = (row_next, row_prev, up, down, swap, up_swap, down_swap)
    for partner in partners:
        pl.semaphore_signal(barrier, inc=1, device_id=partner, device_id_type=MESH)
    pl.semaphore_wait(barrier, len(partners))

    def remote(src, dst, send, recv, i, device, j=None):
        return pltpu.make_async_remote_copy(
            src_ref=src.at[i], dst_ref=dst.at[i if j is None else j], send_sem=send.at[i],
            recv_sem=recv.at[i], device_id=device, device_id_type=MESH,
        )

    def relayed(i):
        return i % 2 == 1

    def swap_copy(src, relay, which, send, i):
        return pltpu.make_async_remote_copy(
            src_ref=src.at[i], dst_ref=relay.at[i // 2], send_sem=send.at[i],
            recv_sem=rel_r.at[which, i // 2], device_id=swap, device_id_type=MESH,
        )

    def forward_copy(relay, which, dst, recv, i):
        return pltpu.make_async_remote_copy(
            src_ref=relay.at[i // 2], dst_ref=dst.at[i], send_sem=rel_s.at[which, i // 2],
            recv_sem=recv.at[i], device_id=up, device_id_type=MESH,
        )

    def send_swaps(src, relay, which, send, i):
        if relayed(i):
            @pl.when(seam)
            def _():
                swap_copy(src, relay, which, send, i).start()

    def send_col(src, dst, send, recv, i):
        copy = remote(src, dst, send, recv, i, col_next)
        if relayed(i):
            pl.when(jnp.logical_not(seam))(copy.start)
        else:
            copy.start()

    def forward(src, relay, which, dst, send, recv, i):
        if relayed(i):
            @pl.when(seam)
            def _():
                swap_copy(src, relay, which, send, i).wait_recv()
                forward_copy(relay, which, dst, recv, i).start()

    for i in range(chunks):
        loads[i].wait()
        send_swaps(xs, x_relay, 0, xc_s, i)
        send_col(xs, xc, xc_s, xc_r, i)
    def send_rows(src, dst, send, recv, condition=None):
        def go():
            for i in range(chunks):
                remote(src, dst, send, recv, i, row_next).start()

        if condition is None:
            go()
        else:
            pl.when(condition)(go)

    def early(src, dst, send, recv):
        @pl.when(landing)
        def _():
            for i in range(chunks):
                if not relayed(i):
                    remote(src, dst, send, recv, i, col_next).wait_recv()

    def wait_col(src, dst, send, recv, i):
        wait = remote(src, dst, send, recv, i, col_next).wait_recv
        if relayed(i):
            wait()
        else:
            pl.when(jnp.logical_not(landing))(wait)

    send_rows(xs, xr, xr_s, xr_r, jnp.logical_or(inner, direct))
    for i in range(chunks):
        remote(xs, xa, xa_s, xa_r, i, two_first).start()

    weights = [jnp.full((1, LANES), num_ref[i].astype(F32), F32) for i in range(3)]
    total = weights[0] + weights[1] + weights[2]
    own, by_row, by_col = (w / total for w in weights)

    def over(i, body):
        def step(t, carry):
            body(pl.ds(pl.multiple_of(t * LANES, LANES), LANES))
            return carry

        lax.fori_loop(0, rows // LANES, step, 0)

    def gradient(which, out):
        def tile(t, carry):
            at = pl.ds(pl.multiple_of(t * TILE, TILE), TILE)
            pre = jnp.dot(tok[at, :], xb[...], preferred_element_type=F32) * factor
            sig = jax.nn.sigmoid(pre)
            hidden = (pre * sig).astype(BF16)
            slope = sig * (1.0 + pre * (1.0 - sig))
            output = jnp.dot(hidden, fro[...], preferred_element_type=F32)
            err = (output - tgt[at, :].astype(F32)).astype(BF16)
            back = jnp.dot(err, frot[...], preferred_element_type=F32)
            place = t * TILE + lax.broadcasted_iota(jnp.int32, (TILE, LANES), 0)
            drawn = jnp.zeros((TILE, LANES), F32)
            for l in range(ids_ref.shape[2] // LANES):
                ids = ids_ref[which, :, l * LANES : (l + 1) * LANES]
                drawn += jnp.where(ids == place, 1.0, 0.0)
            drawn = jnp.sum(drawn, axis=1, keepdims=True)
            bp[at, :] = (back * slope * drawn).astype(BF16)
            return carry

        lax.fori_loop(0, n_pool // TILE, tile, 0)

        def block(t, carry):
            to = pl.ds(pl.multiple_of(t * TILE, TILE), TILE)
            for p in range(split):
                at = pl.ds(pl.multiple_of(t * TILE + p * rows, TILE), TILE)
                for n in range(heads // TILE):
                    g = jnp.dot(tokt[at, :], bp[:, n * TILE : (n + 1) * TILE], preferred_element_type=F32) * factor
                    for l in range(TILE // LANES):
                        out[(n * (TILE // LANES) + l) * split + p, to, :] = g[:, l * LANES : (l + 1) * LANES]
            return carry

        lax.fori_loop(0, rows // TILE, block, 0)

    def store(ref, i, at, value):
        to_rows = pl.ds(at.start + (i % split) * rows, LANES)
        ref[0, 0, to_rows, (i // split) * LANES : (i // split + 1) * LANES] = value

    def put(i, at, value):
        to = pl.ds(at.start + (i % split) * rows, LANES)
        xb[to, (i // split) * LANES : (i // split + 1) * LANES] = value.astype(BF16)

    for i in range(chunks):
        def cast(at, i=i):
            put(i, at, xs[i, at, :])
        over(i, cast)
    tok_load.wait()

    def turn(t, carry):
        at = pl.ds(pl.multiple_of(t * TILE, TILE), TILE)
        tokt[:, at] = tok[at, :].T
        return carry

    lax.fori_loop(0, n_pool // TILE, turn, 0)
    fro_load.wait()
    for t in range(heads // TILE):
        frot[:, t * TILE : (t + 1) * TILE] = fro[t * TILE : (t + 1) * TILE, :].T
    tgt_load.wait()
    ids_load.wait()
    gradient(0, g0)

    def pass_on(i):
        remote(xs, xa, xa_s, xa_r, i, two_first).wait_recv()
        remote(xa, xx, xx_s, xx_r, i, down).start()

    with scope("fwdx"):
        for i in range(chunks):
            forward(xs, x_relay, 0, xc, xc_s, xc_r, i)
    with scope("earlyx"):
        early(xs, xc, xc_s, xc_r)
    send_rows(xs, xr, xr_s, xr_r, jnp.logical_or(landing, through))
    for i in range(chunks):
        send_col(g0, gc, gc_s, gc_r, i)
    with scope("passA"):
        for i in range(chunks // 2):
            pass_on(i)

    for i in range(chunks):
        with scope(f"wx{i}"):
            wait_col(xs, xc, xc_s, xc_r, i)
            remote(xs, xr, xr_s, xr_r, i, row_next).wait_recv()

        def first(at, i=i):
            from_col = by_col * xc[i, at, :]
            mixed = own * xs[i, at, :] + by_row * xr[i, at, :] + from_col
            ws[i, at, :] = mixed + from_col
            put(i, at, mixed - STEP * g0[i, at, :])

        over(i, first)
        send_swaps(g0, g_relay, 1, gc_s, i)
        pl.when(inner)(remote(g0, gr, gr_s, gr_r, i, row_next).start)
    send_rows(g0, gr, gr_s, gr_r, direct)
    send_rows(ws, wr, wr_s, wr_r, inner)
    with scope("grad1"):
        gradient(1, g1)

    with scope("passB"):
        for i in range(chunks // 2, chunks):
            pass_on(i)
    with scope("fwdg"):
        for i in range(chunks):
            forward(g0, g_relay, 1, gc, gc_s, gc_r, i)
    with scope("earlyg"):
        early(g0, gc, gc_s, gc_r)
    send_rows(g0, gr, gr_s, gr_r, jnp.logical_or(landing, through))

    for i in range(chunks):
        with scope(f"wg{i}"):
            wait_col(g0, gc, gc_s, gc_r, i)
            remote(g0, gr, gr_s, gr_r, i, row_next).wait_recv()

        def second(at, i=i):
            g = g0[i, at, :]
            mixed = own * g + by_row * gr[i, at, :] + by_col * gc[i, at, :]
            track = (mixed + g1[i, at, :]) - g
            ts[i, at, :] = track
            q[i, at, :] = STEP * (mixed + track)

        over(i, second)
        send_swaps(ts, t_relay, 2, tc_s, i)
        send_col(ts, tc, tc_s, tc_r, i)

    send_rows(ws, wr, wr_s, wr_r, direct)
    send_rows(ts, tr, tr_s, tr_r, jnp.logical_or(direct, inner))
    with scope("fwdt"):
        for i in range(chunks):
            forward(ts, t_relay, 2, tc, tc_s, tc_r, i)
    with scope("earlyt"):
        early(ts, tc, tc_s, tc_r)
    send_rows(ws, wr, wr_s, wr_r, jnp.logical_or(landing, through))
    send_rows(ts, tr, tr_s, tr_r, jnp.logical_or(landing, through))

    for i in range(chunks):
        with scope(f"ww{i}"):
            remote(ws, wr, wr_s, wr_r, i, row_next).wait_recv()
        with scope(f"w2{i}"):
            remote(xa, xx, xx_s, xx_r, i, down).wait_recv()

        def third(at, i=i):
            new = own * ws[i, at, :] + by_row * wr[i, at, :] + (by_col * by_col) * xx[i, at, :] - q[i, at, :]
            put(i, at, new)
            store(xo, i, at, new)

        over(i, third)
    with scope("grad2"):
        gradient(2, q)

    for i in range(chunks):
        with scope(f"wt{i}"):
            wait_col(ts, tc, tc_s, tc_r, i)
            remote(ts, tr, tr_s, tr_r, i, row_next).wait_recv()

        def last(at, i=i):
            mixed = own * ts[i, at, :] + by_row * tr[i, at, :] + by_col * tc[i, at, :]
            store(to, i, at, (mixed + q[i, at, :]) - g1[i, at, :])

        over(i, last)

    with scope("end"):
        for i in range(chunks):
            remote(xs, xc, xc_s, xc_r, i, col_next).wait_send()
            remote(xs, xr, xr_s, xr_r, i, row_next).wait_send()
            remote(xs, xa, xa_s, xa_r, i, two_first).wait_send()
            remote(xa, xx, xx_s, xx_r, i, down).wait_send()
            remote(ws, wr, wr_s, wr_r, i, row_next).wait_send()
            remote(g0, gc, gc_s, gc_r, i, col_next).wait_send()
            remote(g0, gr, gr_s, gr_r, i, row_next).wait_send()
            remote(ts, tc, tc_s, tc_r, i, col_next).wait_send()
            remote(ts, tr, tr_s, tr_r, i, row_next).wait_send()
            if relayed(i):
                @pl.when(seam)
                def _():
                    forward_copy(x_relay, 0, xc, xc_r, i).wait_send()
                    forward_copy(g_relay, 1, gc, gc_r, i).wait_send()
                    forward_copy(t_relay, 2, tc, tc_r, i).wait_send()


def on_device(value_proj, token_pool, target_pool, batch_ids, frozen_out, numerators):
    depth, heads = value_proj.shape[2:]
    n_pool = token_pool.shape[2]
    ids = batch_ids.reshape(batch_ids.shape[2], 1, batch_ids.shape[3])
    chunks, rows = SPLIT * heads // LANES, depth // SPLIT
    field = pltpu.VMEM((chunks, rows, LANES), F32)
    relay = pltpu.VMEM((chunks // 2, rows, LANES), F32)
    dma = pltpu.SemaphoreType.DMA
    out = pltpu.VMEM(value_proj.shape, F32)
    vmem = pl.BlockSpec(memory_space=pltpu.VMEM)
    hbm = pl.BlockSpec(memory_space=pl.ANY)
    return pl.pallas_call(
        kernel,
        out_shape=(out, out),
        in_specs=[
            pl.BlockSpec(memory_space=pltpu.SMEM), hbm, hbm, hbm,
            hbm, hbm,
        ],
        out_specs=(vmem, vmem),
        scratch_shapes=[field] * 15 + [relay] * 3 + [
            pltpu.VMEM((n_pool, depth), BF16),
            pltpu.VMEM((n_pool, depth), BF16),
            pltpu.VMEM((depth, n_pool), BF16),
            pltpu.VMEM((heads, depth), BF16),
            pltpu.VMEM((depth, heads), BF16),
            pltpu.VMEM((n_pool, heads), BF16),
            pltpu.VMEM((depth, heads), BF16),
            pltpu.VMEM(ids.shape, jnp.int32),
            dma((4,)), dma((chunks,)),
        ] + [dma((chunks,))] * 18 + [dma((3, chunks // 2))] * 2,
        compiler_params=pltpu.CompilerParams(
            collective_id=0, has_side_effects=True, vmem_limit_bytes=58 * 2**20,
        ),
    )(numerators, value_proj, token_pool, target_pool, ids, frozen_out)


def solution(mesh):
    return jax.shard_map(
        on_device,
        mesh=mesh,
        in_specs=(
            P("row", "col", None, None),
            P("row", "col", None, None),
            P("row", "col", None, None),
            P("row", "col", None, None),
            P(),
            P(),
        ),
        out_specs=(P("row", "col", None, None), P("row", "col", None, None)),
        check_vma=False,
    )
```

time: 207 us -> 180 us (0.87)
  the two profiles are of different devices: /device:TPU:34 before, /device:TPU:24 now
where the time goes in v2:
time: 180 us; the launch traced here: 179 us
  Pallas kernels  176 us (98%)
  local copies, waits for them, and re-layouts  2.64 us (1%)
    pallas_call x1, Pallas kernels, on_device(): pl.pallas_call(kernel, out_shape=(out, out), in_specs=[pl.BlockSpec(memor...  176 us

profile of v2, /device:TPU:24, one launch (start us, length us, event | category | flops | bytes accessed | tf_op | source)
XLA Modules:
  0.0 178.8 jit_solution(7187822918132167170)
XLA Ops:
  0.6 175.5 %shard_map.77 = (f32[1,1,1024,512]{3,2,1,0:T(8,128)S(1)}, f32[1,1,1024,512]{3,2,1,0:T(8,128)S(1)}) custom-call(s32[3]{0:T(128)} %num_ref.1, f32[1,1,1024,512]{3,2,1,0:T(8,128)} %x_hbm.1, bf16[1,1,1536,1024]{3,2,1,0:T(8,128)(2,1)} %tok_hbm.1, bf16[1,1,1536,1024]{3,2,1,0:T(8,128)(2,1)} %tgt_hbm.1, s32[3,1,1536]{2,1,0:T(1,128)} %bitcast.1, ...), custom_call_target="tpu_custom_call" | custom-call | tf_op jit(solution)/shard_map/pallas_call | solution.py:351
  176.2 1.3 copy.10
  177.5 1.3 copy.11

commit v3 on v2

--- a/solution.py
+++ b/solution.py
@@ -12,6 +12,8 @@
 BF16 = jnp.bfloat16
 STEP = 0.2
 SPLIT = 2
+FIRST = 3
+ROUND = 4
 LANES = 128
 TILE = 256
 
@@ -20,12 +22,12 @@
     num_ref, x_hbm, tok_hbm, tgt_hbm, ids_hbm, fro_hbm,
     xo, to,
     xs, xr, xc, xa, xx, ws, wr, g0, gr, gc, g1, ts, tr, tc, q,
-    x_relay, g_relay, t_relay,
+    x_relay, g_relay, t_relay, w_relay,
     tok, tgt, tokt, fro, frot, bp, xb, ids_ref,
     load_sem, x_sem,
     xr_s, xr_r, xc_s, xc_r, xa_s, xa_r, xx_s, xx_r, wr_s, wr_r,
     gr_s, gr_r, gc_s, gc_r, tr_s, tr_r, tc_s, tc_r,
-    rel_s, rel_r,
+    rel_s, rel_r, via_s, via_r,
 ):
     chunks, rows, _ = xs.shape
     split = tok.shape[1] // rows
@@ -51,6 +53,10 @@
     down = (r, half + lax.rem(y + 3, 4))
     up_swap = (r, lax.rem(up[1] + 4, 8))
     down_swap = (r, lax.rem(down[1] + 4, 8))
+    mate = (r, jnp.where(lax.rem(y, 2) == 0, up[1], down[1]))
+    mate_next = (row_next[0], mate[1])
+    mate_prev = (row_prev[0], mate[1])
+    leaves = lax.rem(r, 2) == 1
     two_first = (r, jnp.where(y >= 2, down_swap[1], down[1]))
 
     def window(ref, i):
@@ -72,7 +78,7 @@
     tgt_load.start()
 
     barrier = pltpu.get_barrier_semaphore()
-    partners = (row_next, row_prev, up, down, swap, up_swap, down_swap)
+    partners = (row_next, row_prev, up, down, swap, up_swap, down_swap, mate_next, mate_prev)
     for partner in partners:
         pl.semaphore_signal(barrier, inc=1, device_id=partner, device_id_type=MESH)
     pl.semaphore_wait(barrier, len(partners))
@@ -221,6 +227,42 @@
     ids_load.wait()
     gradient(0, g0)
 
+    def via_copy(i):
+        return pltpu.make_async_remote_copy(
+            src_ref=ws.at[i], dst_ref=w_relay.at[i], send_sem=wr_s.at[i],
+            recv_sem=via_r.at[i], device_id=mate_next, device_id_type=MESH,
+        )
+
+    def via_forward(i):
+        return pltpu.make_async_remote_copy(
+            src_ref=w_relay.at[i], dst_ref=wr.at[i], send_sem=via_s.at[i],
+            recv_sem=wr_r.at[i], device_id=mate, device_id_type=MESH,
+        )
+
+    around = jnp.logical_and(outer, leaves)
+    carries = jnp.logical_and(inner, jnp.logical_not(leaves))
+
+    def send_around():
+        @pl.when(around)
+        def _():
+            for i in range(ROUND):
+                via_copy(i).start()
+
+    def carry_on():
+        @pl.when(carries)
+        def _():
+            for i in range(ROUND):
+                via_copy(i).wait_recv()
+                via_forward(i).start()
+
+    def send_rest(condition):
+        @pl.when(condition)
+        def _():
+            for i in range(ROUND):
+                pl.when(jnp.logical_not(around))(remote(ws, wr, wr_s, wr_r, i, row_next).start)
+            for i in range(ROUND, chunks):
+                remote(ws, wr, wr_s, wr_r, i, row_next).start()
+
     def pass_on(i):
         remote(xs, xa, xa_s, xa_r, i, two_first).wait_recv()
         remote(xa, xx, xx_s, xx_r, i, down).start()
@@ -252,7 +294,6 @@
         send_swaps(g0, g_relay, 1, gc_s, i)
         pl.when(inner)(remote(g0, gr, gr_s, gr_r, i, row_next).start)
     send_rows(g0, gr, gr_s, gr_r, direct)
-    send_rows(ws, wr, wr_s, wr_r, inner)
     with scope("grad1"):
         gradient(1, g1)
 
@@ -265,6 +306,7 @@
     with scope("earlyg"):
         early(g0, gc, gc_s, gc_r)
     send_rows(g0, gr, gr_s, gr_r, jnp.logical_or(landing, through))
+    send_around()
 
     for i in range(chunks):
         with scope(f"wg{i}"):
@@ -280,17 +322,32 @@
 
         over(i, second)
         send_swaps(ts, t_relay, 2, tc_s, i)
-        send_col(ts, tc, tc_s, tc_r, i)
-
-    send_rows(ws, wr, wr_s, wr_r, direct)
+        if i < FIRST:
+            send_col(ts, tc, tc_s, tc_r, i)
+        else:
+            @pl.when(outer)
+            def _(i=i):
+                send_col(ts, tc, tc_s, tc_r, i)
+
+
+    send_rest(jnp.logical_or(direct, landing))
+    send_rows(ws, wr, wr_s, wr_r, inner)
     send_rows(ts, tr, tr_s, tr_r, jnp.logical_or(direct, inner))
     with scope("fwdt"):
         for i in range(chunks):
             forward(ts, t_relay, 2, tc, tc_s, tc_r, i)
     with scope("earlyt"):
         early(ts, tc, tc_s, tc_r)
-    send_rows(ws, wr, wr_s, wr_r, jnp.logical_or(landing, through))
+    send_rest(through)
     send_rows(ts, tr, tr_s, tr_r, jnp.logical_or(landing, through))
+
+    with scope("carry"):
+        carry_on()
+
+    @pl.when(inner)
+    def _():
+        for i in range(FIRST, chunks):
+            send_col(ts, tc, tc_s, tc_r, i)
 
     for i in range(chunks):
         with scope(f"ww{i}"):
@@ -335,6 +392,11 @@
                     forward_copy(x_relay, 0, xc, xc_r, i).wait_send()
                     forward_copy(g_relay, 1, gc, gc_r, i).wait_send()
                     forward_copy(t_relay, 2, tc, tc_r, i).wait_send()
+
+        @pl.when(carries)
+        def _():
+            for i in range(ROUND):
+                via_forward(i).wait_send()
 
 
 def on_device(value_proj, token_pool, target_pool, batch_ids, frozen_out, numerators):
@@ -357,6 +419,7 @@
         ],
         out_specs=(vmem, vmem),
         scratch_shapes=[field] * 15 + [relay] * 3 + [
+            pltpu.VMEM((ROUND, rows, LANES), F32),
             pltpu.VMEM((n_pool, depth), BF16),
             pltpu.VMEM((n_pool, depth), BF16),
             pltpu.VMEM((depth, n_pool), BF16),
@@ -366,7 +429,7 @@
             pltpu.VMEM((depth, heads), BF16),
             pltpu.VMEM(ids.shape, jnp.int32),
             dma((4,)), dma((chunks,)),
-        ] + [dma((chunks,))] * 18 + [dma((3, chunks // 2))] * 2,
+        ] + [dma((chunks,))] * 18 + [dma((3, chunks // 2))] * 2 + [dma((ROUND,))] * 2,
         compiler_params=pltpu.CompilerParams(
             collective_id=0, has_side_effects=True, vmem_limit_bytes=58 * 2**20,
         ),

time: 180 us -> 168 us (0.933)
  Pallas kernels: 176 us -> 165 us
    pallas_call x1, Pallas kernels: 176 us -> 165 us  [on_device(): pl.pallas_call(kernel, out_shape=(out, out), in_specs=[pl.BlockSpec(memor...]
where the time goes in v3:
time: 168 us
  Pallas kernels  165 us (98%)
  local copies, waits for them, and re-layouts  2.64 us (2%)
    pallas_call x1, Pallas kernels, on_device(): pl.pallas_call(kernel, out_shape=(out, out), in_specs=[pl.BlockSpec(memor...  165 us

profile of v3, /device:TPU:24, one launch (start us, length us, event | category | flops | bytes accessed | tf_op | source)
XLA Modules:
  0.0 168.1 jit_solution(14311523069089257196)
XLA Ops:
  0.6 164.8 %shard_map.77 = (f32[1,1,1024,512]{3,2,1,0:T(8,128)S(1)}, f32[1,1,1024,512]{3,2,1,0:T(8,128)S(1)}) custom-call(s32[3]{0:T(128)} %num_ref.1, f32[1,1,1024,512]{3,2,1,0:T(8,128)} %x_hbm.1, bf16[1,1,1536,1024]{3,2,1,0:T(8,128)(2,1)} %tok_hbm.1, bf16[1,1,1536,1024]{3,2,1,0:T(8,128)(2,1)} %tgt_hbm.1, s32[3,1,1536]{2,1,0:T(1,128)} %bitcast.1, ...), custom_call_target="tpu_custom_call" | custom-call | tf_op jit(solution)/shard_map/pallas_call | solution.py:413
  165.5 1.3 copy.10
  166.8 1.3 copy.11

commit v4 on v3

--- a/solution.py
+++ b/solution.py
@@ -12,8 +12,10 @@
 BF16 = jnp.bfloat16
 STEP = 0.2
 SPLIT = 2
+AHEAD = 6
+BEHIND = 7
 FIRST = 3
-ROUND = 4
+ROUND = 5
 LANES = 128
 TILE = 256
 
@@ -142,18 +144,18 @@
         @pl.when(landing)
         def _():
             for i in range(chunks):
-                if not relayed(i):
+                if i < AHEAD and not relayed(i):
                     remote(src, dst, send, recv, i, col_next).wait_recv()
 
     def wait_col(src, dst, send, recv, i):
         wait = remote(src, dst, send, recv, i, col_next).wait_recv
-        if relayed(i):
+        if relayed(i) or i >= AHEAD:
             wait()
         else:
             pl.when(jnp.logical_not(landing))(wait)
 
     send_rows(xs, xr, xr_s, xr_r, jnp.logical_or(inner, direct))
-    for i in range(chunks):
+    for i in range(chunks // 2):
         remote(xs, xa, xa_s, xa_r, i, two_first).start()
 
     weights = [jnp.full((1, LANES), num_ref[i].astype(F32), F32) for i in range(3)]
@@ -270,14 +272,18 @@
     with scope("fwdx"):
         for i in range(chunks):
             forward(xs, x_relay, 0, xc, xc_s, xc_r, i)
+            if i == BEHIND:
+                send_rows(xs, xr, xr_s, xr_r, through)
     with scope("earlyx"):
         early(xs, xc, xc_s, xc_r)
-    send_rows(xs, xr, xr_s, xr_r, jnp.logical_or(landing, through))
+    send_rows(xs, xr, xr_s, xr_r, landing)
     for i in range(chunks):
         send_col(g0, gc, gc_s, gc_r, i)
     with scope("passA"):
         for i in range(chunks // 2):
             pass_on(i)
+    for i in range(chunks // 2, chunks):
+        remote(xs, xa, xa_s, xa_r, i, two_first).start()
 
     for i in range(chunks):
         with scope(f"wx{i}"):
@@ -297,16 +303,18 @@
     with scope("grad1"):
         gradient(1, g1)
 
+    with scope("fwdg"):
+        for i in range(chunks):
+            forward(g0, g_relay, 1, gc, gc_s, gc_r, i)
+            if i == BEHIND:
+                send_rows(g0, gr, gr_s, gr_r, through)
+    with scope("earlyg"):
+        early(g0, gc, gc_s, gc_r)
+    send_rows(g0, gr, gr_s, gr_r, landing)
+    send_around()
     with scope("passB"):
         for i in range(chunks // 2, chunks):
             pass_on(i)
-    with scope("fwdg"):
-        for i in range(chunks):
-            forward(g0, g_relay, 1, gc, gc_s, gc_r, i)
-    with scope("earlyg"):
-        early(g0, gc, gc_s, gc_r)
-    send_rows(g0, gr, gr_s, gr_r, jnp.logical_or(landing, through))
-    send_around()
 
     for i in range(chunks):
         with scope(f"wg{i}"):
@@ -336,10 +344,12 @@
     with scope("fwdt"):
         for i in range(chunks):
             forward(ts, t_relay, 2, tc, tc_s, tc_r, i)
+            if i == BEHIND:
+                send_rest(through)
+                send_rows(ts, tr, tr_s, tr_r, through)
     with scope("earlyt"):
         early(ts, tc, tc_s, tc_r)
-    send_rest(through)
-    send_rows(ts, tr, tr_s, tr_r, jnp.logical_or(landing, through))
+    send_rows(ts, tr, tr_s, tr_r, landing)
 
     with scope("carry"):
         carry_on()

time: 168 us -> 167 us (level); the launches traced: 168 us -> 165 us
  Pallas kernels: 165 us -> 162 us
    pallas_call x1, Pallas kernels: 165 us -> 162 us  [on_device(): pl.pallas_call(kernel, out_shape=(out, out), in_specs=[pl.BlockSpec(memor...]
where the time goes in v4:
time: 167 us; the launch traced here: 165 us
  Pallas kernels  162 us (97%)
  local copies, waits for them, and re-layouts  2.64 us (2%)
    pallas_call x1, Pallas kernels, on_device(): pl.pallas_call(kernel, out_shape=(out, out), in_specs=[pl.BlockSpec(memor...  162 us

profile of v4, /device:TPU:24, one launch (start us, length us, event | category | flops | bytes accessed | tf_op | source)
XLA Modules:
  0.0 165.3 jit_solution(5133206590338857204)
XLA Ops:
  0.6 162.0 %shard_map.77 = (f32[1,1,1024,512]{3,2,1,0:T(8,128)S(1)}, f32[1,1,1024,512]{3,2,1,0:T(8,128)S(1)}) custom-call(s32[3]{0:T(128)} %num_ref.1, f32[1,1,1024,512]{3,2,1,0:T(8,128)} %x_hbm.1, bf16[1,1,1536,1024]{3,2,1,0:T(8,128)(2,1)} %tok_hbm.1, bf16[1,1,1536,1024]{3,2,1,0:T(8,128)(2,1)} %tgt_hbm.1, s32[3,1,1536]{2,1,0:T(1,128)} %bitcast.1, ...), custom_call_target="tpu_custom_call" | custom-call | tf_op jit(solution)/shard_map/pallas_call | solution.py:423
  162.7 1.3 copy.10
  164.0 1.3 copy.11
